TPU v7x, 8 devices: a whole 2x2x1 slice. The times are simulated.
8 devices in a mesh: z: 2 (over z, y), y: 2 (over x), xc: 2 (over core).
Axes of the slice: x: 2, y: 2, z: 1, core: 2. Of those that a mesh axis runs over, the one named last changes fastest.
Arguments:
- tokens_x: bfloat16 [65536, 512], P(('z', 'y', 'xc'))
- grad_y: bfloat16 [65536, 512], P(('z', 'y', 'xc'))
- w_one: bfloat16 [512, 2048], replicated
- w_two: bfloat16 [2048, 512], replicated
- w_three: bfloat16 [512, 2048], replicated
- w_four: bfloat16 [2048, 512], replicated
Outputs:
- output 1: float32 [512, 2048], replicated
- output 2: float32 [2048, 512], replicated
- output 3: float32 [512, 2048], replicated
- output 4: float32 [2048, 512], replicated
All inputs are finite; a program needn't handle non-finite values.
Results may differ from a plain program's by a relative error of at most 0.00328.
Values are sent between devices in bfloat16 or wider.
A program may use at most 1 GiB of HBM per device.

v0:
```python
import math
import jax
import jax.numpy as jnp
from jax import lax
from jax.sharding import PartitionSpec as P

GELU_SCALE = math.sqrt(2.0 / math.pi)
GELU_CUBIC = 0.044715


def gelu_value(pre_act):
    return 0.5 * pre_act * (1.0 + jnp.tanh(GELU_SCALE * (pre_act + GELU_CUBIC * pre_act * pre_act * pre_act)))


def gelu_grad(pre_act):
    tanh_val = jnp.tanh(GELU_SCALE * (pre_act + GELU_CUBIC * pre_act * pre_act * pre_act))
    return 0.5 * (1.0 + tanh_val) + 0.5 * pre_act * (1.0 - tanh_val * tanh_val) * GELU_SCALE * (1.0 + 3.0 * GELU_CUBIC * pre_act * pre_act)


def solution(mesh):
    n_dev = math.prod(mesh.shape.values())
    batch_spec = P(("z", "y", "xc"), None)
    whole_spec = P(None, None)

    def reduce_grad(local_grad):
        reduced = lax.psum_scatter(local_grad, "xc", scatter_dimension=0, tiled=True)
        reduced = lax.psum_scatter(reduced, "y", scatter_dimension=0, tiled=True)
        reduced = lax.psum(reduced, "z")
        reduced = lax.all_gather(reduced, "y", axis=0, tiled=True)
        reduced = lax.all_gather(reduced, "xc", axis=0, tiled=True)
        return reduced / n_dev

    def device_step(x_loc, g_loc, w_one, w_two, w_three, w_four):
        a_one = jnp.dot(x_loc, w_one, preferred_element_type=jnp.float32).astype(jnp.bfloat16)
        h_one = gelu_value(a_one.astype(jnp.float32)).astype(jnp.bfloat16)
        h_two = (jnp.dot(h_one, w_two, preferred_element_type=jnp.float32) + x_loc.astype(jnp.float32)).astype(jnp.bfloat16)
        a_three = jnp.dot(h_two, w_three, preferred_element_type=jnp.float32).astype(jnp.bfloat16)
        h_three = gelu_value(a_three.astype(jnp.float32)).astype(jnp.bfloat16)
        grad_w4 = reduce_grad(jnp.einsum("nf,nd->fd", h_three, g_loc, preferred_element_type=jnp.float32))
        d_a3 = (jnp.einsum("nd,fd->nf", g_loc, w_four, preferred_element_type=jnp.float32) * gelu_grad(a_three.astype(jnp.float32))).astype(jnp.bfloat16)
        grad_w3 = reduce_grad(jnp.einsum("nd,nf->df", h_two, d_a3, preferred_element_type=jnp.float32))
        d_h2 = (jnp.einsum("nf,df->nd", d_a3, w_three, preferred_element_type=jnp.float32) + g_loc.astype(jnp.float32)).astype(jnp.bfloat16)
        grad_w2 = reduce_grad(jnp.einsum("nf,nd->fd", h_one, d_h2, preferred_element_type=jnp.float32))
        d_a1 = (jnp.einsum("nd,fd->nf", d_h2, w_two, preferred_element_type=jnp.float32) * gelu_grad(a_one.astype(jnp.float32))).astype(jnp.bfloat16)
        grad_w1 = reduce_grad(jnp.einsum("nd,nf->df", x_loc, d_a1, preferred_element_type=jnp.float32))
        return grad_w1, grad_w2, grad_w3, grad_w4

    return jax.shard_map(
        device_step,
        mesh=mesh,
        in_specs=(batch_spec, batch_spec, whole_spec, whole_spec, whole_spec, whole_spec),
        out_specs=(whole_spec, whole_spec, whole_spec, whole_spec),
        check_vma=False,
    )
```

profile of v0, /device:TPU:0, one launch (start us, length us, event | category | flops | bytes accessed | tf_op | source)
XLA Modules:
  0.0 783.2 jit_solution(16254520722067976013)
XLA Ops:
  7.2 0.0 reduce-scatter.17.cloned.1.call-start
  7.2 24.6 %convolution_convert_fusion.1 = bf16[8192,2048]{1,0:T(8,128)(2,1)} fusion(bf16[8192,512]{1,0:T(8,128)(2,1)} %param.6, bf16[512,2048]{1,0:T(8,128)(2,1)} %param.8), kind=kOutput, calls=%fused_computation.38 | convolution fusion | flops 17196646400 | bytes 44040192 | tf_op jit(solution)/shard_map/dot_general | solution.py:34
  31.9 33.7 %add_convert_fusion.1 = bf16[8192,512]{1,0:T(8,128)(2,1)} fusion(bf16[8192,512]{1,0:T(8,128)(2,1)} %param.6, bf16[2048,512]{1,0:T(8,128)(2,1)} %param.9, bf16[8192,2048]{1,0:T(8,128)(2,1)} %convolution_convert_fusion.1), kind=kOutput, calls=%fused_computation.41 | convolution fusion | flops 17360224256 | bytes 52428800 | tf_op jit(solution)/shard_map/dot_general | solution.py:36
  65.6 24.8 %convolution_convert_fusion = bf16[8192,2048]{1,0:T(8,128)(2,1)} fusion(bf16[8192,512]{1,0:T(8,128)(2,1)} %add_convert_fusion.1, bf16[512,2048]{1,0:T(8,128)(2,1)S(1)} %copy-done), kind=kOutput, calls=%fused_computation.37 | convolution fusion | flops 17196646400 | bytes 44040192 | tf_op jit(solution)/shard_map/dot_general | solution.py:37
  90.4 57.7 %fusion.8 = bf16[8192,2048]{1,0:T(8,128)(2,1)} fusion(bf16[8192,2048]{1,0:T(8,128)(2,1)} %convolution_convert_fusion, bf16[8192,512]{1,0:T(8,128)(2,1)} %param.7, bf16[2048,512]{1,0:T(8,128)(2,1)} %param.11), kind=kOutput, calls=%fused_computation.22 | convolution fusion | flops 17515413504 | bytes 77594624 | tf_op jit(solution)/shard_map/nd,fd->nf/dot_general | solution.py:40
  148.2 25.1 %fusion.38 = f32[512,2048]{0,1:T(8,128)} fusion(bf16[8192,512]{1,0:T(8,128)(2,1)} %add_convert_fusion.1, bf16[8192,2048]{1,0:T(8,128)(2,1)} %fusion.8), kind=kOutput, calls=%fused_computation.57 | convolution fusion | flops 17179869184 | bytes 46137344 | tf_op jit(solution)/shard_map/nd,nf->df/dot_general | solution.py:41
  173.3 0.0 reduce-scatter.21.cloned.1.call-start
  173.3 35.5 %fusion.22 = f32[2048,512]{1,0:T(8,128)} fusion(bf16[8192,512]{1,0:T(8,128)(2,1)} %param.7, bf16[8192,2048]{1,0:T(8,128)(2,1)} %convolution_convert_fusion), kind=kOutput, calls=%fused_computation.36 | convolution fusion | flops 17347641344 | bytes 46137344 | tf_op jit(solution)/shard_map/nf,nd->fd/dot_general | solution.py:39
  208.8 0.0 reduce-scatter.9.cloned.1.call-start
  208.9 25.3 %add_convert_fusion = bf16[8192,512]{1,0:T(8,128)(2,1)} fusion(bf16[8192,512]{1,0:T(8,128)(2,1)} %param.7, bf16[8192,2048]{1,0:T(8,128)(2,1)} %fusion.8, bf16[512,2048]{1,0:T(8,128)(2,1)S(1)} %copy-done), kind=kOutput, calls=%fused_computation.40 | convolution fusion | flops 17192452096 | bytes 52428800 | tf_op jit(solution)/shard_map/nf,df->nd/dot_general | solution.py:42
  234.2 56.8 %fusion.15.clone.6 = bf16[8192,2048]{1,0:T(8,128)(2,1)} fusion(bf16[8192,2048]{1,0:T(8,128)(2,1)} %convolution_convert_fusion.1, bf16[8192,512]{1,0:T(8,128)(2,1)} %add_convert_fusion, bf16[2048,512]{1,0:T(8,128)(2,1)S(1)} %copy-done.2), kind=kOutput, calls=%fused_computation.29.clone.clone.clone.clone.clone.1 | convolution fusion | flops 17515413504 | bytes 77594624 | tf_op jit(solution)/shard_map/nd,fd->nf/dot_general | solution.py:44
  291.0 22.4 %fusion.25 = f32[512,2048]{0,1:T(8,128)} fusion(bf16[8192,512]{1,0:T(8,128)(2,1)S(1)} %copy-done.1, bf16[8192,2048]{1,0:T(8,128)(2,1)} %fusion.15.clone.6), kind=kOutput, calls=%fused_computation.42 | convolution fusion | flops 17179869184 | bytes 46137344 | tf_op jit(solution)/shard_map/nd,nf->df/dot_general | solution.py:45
  313.4 0.0 reduce-scatter.13.cloned.1.call-start
  313.5 35.6 %fusion.35 = f32[2048,512]{1,0:T(8,128)} fusion(bf16[8192,512]{1,0:T(8,128)(2,1)} %add_convert_fusion, bf16[8192,2048]{1,0:T(8,128)(2,1)} %convolution_convert_fusion.1), kind=kOutput, calls=%fused_computation.56 | convolution fusion | flops 17347641344 | bytes 46137344 | tf_op jit(solution)/shard_map/nf,nd->fd/dot_general | solution.py:43
  349.1 0.0 reduce-scatter.19.cloned.1.call-start
  349.2 0.5 reduce-scatter.19.cloned.1.call-update
  349.8 0.5 reduce-scatter.23.cloned.1.call-update
  350.4 0.7 reduce-scatter.11.cloned.1.call-update
  351.0 0.0 reduce-scatter.15.cloned.1.call-start
  351.1 9.8 %reduce-scatter.13.cloned.1.call-done = f32[1024,512]{1,0:T(8,128)} async-done(((f32[2048,512]{1,0:T(8,128)}), f32[1024,512]{1,0:T(8,128)}) %reduce-scatter.13.cloned.1.call-update) | async-done | bytes 2097168 | tf_op jit(solution)/shard_map/reduce_scatter | solution.py:26
  360.9 0.0 all-reduce.3.cloned.1.call-start
  360.9 32.2 %reduce-scatter.19.cloned.1.call-done = f32[128,2048]{0,1:T(8,128)} async-done(((f32[256,2048]{0,1:T(8,128)}), f32[128,2048]{0,1:T(8,128)}) %reduce-scatter.19.cloned.1.call-update) | async-done | bytes 1048592 | tf_op jit(solution)/shard_map/reduce_scatter | solution.py:27
  393.1 31.1 %reduce-scatter.23.cloned.1.call-done = f32[512,512]{1,0:T(8,128)} async-done(((f32[1024,512]{1,0:T(8,128)}), f32[512,512]{1,0:T(8,128)}) %reduce-scatter.23.cloned.1.call-update) | async-done | bytes 1048592 | tf_op jit(solution)/shard_map/reduce_scatter | solution.py:27
  424.2 31.3 %reduce-scatter.11.cloned.1.call-done = f32[128,2048]{0,1:T(8,128)} async-done(((f32[256,2048]{0,1:T(8,128)}), f32[128,2048]{0,1:T(8,128)}) %reduce-scatter.11.cloned.1.call-update) | async-done | bytes 1048592 | tf_op jit(solution)/shard_map/reduce_scatter | solution.py:27
  455.5 31.3 %reduce-scatter.15.cloned.1.call-done = f32[512,512]{1,0:T(8,128)} async-done(((f32[1024,512]{1,0:T(8,128)}), f32[512,512]{1,0:T(8,128)}) %reduce-scatter.15.cloned.1.call-update) | async-done | bytes 1048592 | tf_op jit(solution)/shard_map/reduce_scatter | solution.py:27
  486.8 0.0 all-gather.9.cloned.1.call-start
  486.8 104.6 %all-reduce.3.cloned.1.call-done = (f32[128,2048]{0,1:T(8,128)}, f32[512,512]{1,0:T(8,128)}, f32[128,2048]{0,1:T(8,128)}, f32[512,512]{1,0:T(8,128)}) async-done(((f32[128,2048]{0,1:T(8,128)}, f32[512,512]{1,0:T(8,128)}, f32[128,2048]{0,1:T(8,128)}, f32[512,512]{1,0:T(8,128)}), (f32[128,2048]{0,1:T(8,128)}, f32[512,512]{1,0:T(8,128)}, f32[128,2048]{0,1:T(8,128)}, ...) | async-done | bytes 4194320 | tf_op jit(solution)/shard_map/psum | solution.py:28
  591.5 0.0 all-gather.17.cloned.1.call-start
  591.5 0.7 all-gather.17.cloned.1.call-update
  592.2 0.0 all-gather.13.cloned.1.call-start
  592.2 0.5 all-gather.13.cloned.1.call-update
  592.8 0.0 all-gather.21.cloned.1.call-start
  592.8 0.7 all-gather.21.cloned.1.call-update
  593.6 29.4 %all-gather.9.cloned.1.call-done = f32[256,2048]{0,1:T(8,128)} async-done(((f32[128,2048]{0,1:T(8,128)}), f32[256,2048]{0,1:T(8,128)}) %all-gather.9.cloned.1.call-update) | async-done | bytes 2097168 | tf_op jit(solution)/shard_map/all_gather | solution.py:29
  623.0 31.6 %all-gather.17.cloned.1.call-done = f32[256,2048]{0,1:T(8,128)} async-done(((f32[128,2048]{0,1:T(8,128)}), f32[256,2048]{0,1:T(8,128)}) %all-gather.17.cloned.1.call-update) | async-done | bytes 2097168 | tf_op jit(solution)/shard_map/all_gather | solution.py:29
  654.7 31.5 %all-gather.13.cloned.1.call-done = f32[1024,512]{1,0:T(8,128)} async-done(((f32[512,512]{1,0:T(8,128)}), f32[1024,512]{1,0:T(8,128)}) %all-gather.13.cloned.1.call-update) | async-done | bytes 2097168 | tf_op jit(solution)/shard_map/all_gather | solution.py:29
  686.1 0.0 all-gather.23.cloned.1.call-start
  686.2 31.6 %all-gather.21.cloned.1.call-done = f32[1024,512]{1,0:T(8,128)} async-done(((f32[512,512]{1,0:T(8,128)}), f32[1024,512]{1,0:T(8,128)}) %all-gather.21.cloned.1.call-update) | async-done | bytes 2097168 | tf_op jit(solution)/shard_map/all_gather | solution.py:29
  717.8 12.6 %all-gather.11.cloned.1.call-done = f32[512,2048]{0,1:T(8,128)} async-done(((f32[256,2048]{0,1:T(8,128)}), f32[512,2048]{0,1:T(8,128)}) %all-gather.11.cloned.1.call-update) | async-done | bytes 4194320 | tf_op jit(solution)/shard_map/all_gather | solution.py:30
  730.4 4.7 broadcast_multiply_fusion.3
  735.1 5.3 copy.11
  740.5 3.7 all-gather.19.cloned.1.call-done
  744.2 4.7 broadcast_multiply_fusion.2
  748.9 5.3 copy.12
  754.3 3.8 all-gather.15.cloned.1.call-done
  758.0 4.7 broadcast_multiply_fusion.1
  762.7 9.1 %all-gather.23.cloned.1.call-done = f32[2048,512]{1,0:T(8,128)} async-done(((f32[1024,512]{1,0:T(8,128)}), f32[2048,512]{1,0:T(8,128)}) %all-gather.23.cloned.1.call-update) | async-done | bytes 4194320 | tf_op jit(solution)/shard_map/all_gather | solution.py:30
  771.8 4.7 broadcast_multiply_fusion
  (25 shorter events, 0.4 us)
Async XLA Ops:
  7.2 58.4 %copy-start = (bf16[512,2048]{1,0:T(8,128)(2,1)S(1)}, bf16[512,2048]{1,0:T(8,128)(2,1)}, u32[]{:S(2)}) copy-start(bf16[512,2048]{1,0:T(8,128)(2,1)} %param.10) | copy-start | bytes 6291460
  7.2 342.0 %reduce-scatter.17.cloned.1.call-start = ((), (), s32[]{:S(2)}) async-start(), calls=%async_computation.16 | async-start | bytes 6291456 | tf_op jit(solution)/shard_map/reduce_scatter | solution.py:26
  173.3 176.5 %reduce-scatter.21.cloned.1.call-start = ((), (), s32[]{:S(2)}) async-start(), calls=%async_computation.20 | async-start | bytes 6291456 | tf_op jit(solution)/shard_map/reduce_scatter | solution.py:26
  208.8 141.5 %reduce-scatter.9.cloned.1.call-start = ((), (), s32[]{:S(2)}) async-start(), calls=%async_computation.8 | async-start | bytes 6291456 | tf_op jit(solution)/shard_map/reduce_scatter | solution.py:26
  208.9 25.3 %copy-start.2 = (bf16[2048,512]{1,0:T(8,128)(2,1)S(1)}, bf16[2048,512]{1,0:T(8,128)(2,1)}, u32[]{:S(2)}) copy-start(bf16[2048,512]{1,0:T(8,128)(2,1)} %param.9) | copy-start | bytes 6291460
  234.2 56.8 %copy-start.1 = (bf16[8192,512]{1,0:T(8,128)(2,1)S(1)}, bf16[8192,512]{1,0:T(8,128)(2,1)}, u32[]{:S(2)}) copy-start(bf16[8192,512]{1,0:T(8,128)(2,1)} %param.6) | copy-start | bytes 25165828
  313.4 47.5 %reduce-scatter.13.cloned.1.call-start = ((), (), s32[]{:S(2)}) async-start(), calls=%async_computation.12 | async-start | bytes 6291456 | tf_op jit(solution)/shard_map/reduce_scatter | solution.py:26
  349.1 44.0 %reduce-scatter.19.cloned.1.call-start = ((), (), s32[]{:S(2)}) async-start(), calls=%async_computation.17 | async-start | bytes 3145728 | tf_op jit(solution)/shard_map/reduce_scatter | solution.py:27
  349.7 74.5 %reduce-scatter.23.cloned.1.call-start = ((), (), s32[]{:S(2)}) async-start(), calls=%async_computation.21 | async-start | bytes 3145728 | tf_op jit(solution)/shard_map/reduce_scatter | solution.py:27
  350.3 105.2 %reduce-scatter.11.cloned.1.call-start = ((), (), s32[]{:S(2)}) async-start(), calls=%async_computation.9 | async-start | bytes 3145728 | tf_op jit(solution)/shard_map/reduce_scatter | solution.py:27
  351.0 135.7 %reduce-scatter.15.cloned.1.call-start = ((), (), s32[]{:S(2)}) async-start(), calls=%async_computation.13 | async-start | bytes 3145728 | tf_op jit(solution)/shard_map/reduce_scatter | solution.py:27
  360.9 230.5 %all-reduce.3.cloned.1.call-start = ((), (), s32[]{:S(2)}) async-start(), calls=%async_computation.24 | async-start | bytes 8388608 | tf_op jit(solution)/shard_map/psum | solution.py:28
  486.8 136.1 %all-gather.9.cloned.1.call-start = ((), (), s32[]{:S(2)}) async-start(), calls=%async_computation.10 | async-start | bytes 3145728 | tf_op jit(solution)/shard_map/all_gather | solution.py:29
  591.5 63.1 %all-gather.17.cloned.1.call-start = ((), (), s32[]{:S(2)}) async-start(), calls=%async_computation.18 | async-start | bytes 3145728 | tf_op jit(solution)/shard_map/all_gather | solution.py:29
  592.2 93.9 %all-gather.13.cloned.1.call-start = ((), (), s32[]{:S(2)}) async-start(), calls=%async_computation.14 | async-start | bytes 3145728 | tf_op jit(solution)/shard_map/all_gather | solution.py:29
  592.8 125.0 %all-gather.21.cloned.1.call-start = ((), (), s32[]{:S(2)}) async-start(), calls=%async_computation.22 | async-start | bytes 3145728 | tf_op jit(solution)/shard_map/all_gather | solution.py:29
  593.5 136.9 %all-gather.11.cloned.1.call-start = ((), (), s32[]{:S(2)}) async-start(), calls=%async_computation.11 | async-start | bytes 6291456 | tf_op jit(solution)/shard_map/all_gather | solution.py:30
  623.0 121.3 %all-gather.19.cloned.1.call-start = ((), (), s32[]{:S(2)}) async-start(), calls=%async_computation.19 | async-start | bytes 6291456 | tf_op jit(solution)/shard_map/all_gather | solution.py:30
  654.6 103.4 %all-gather.15.cloned.1.call-start = ((), (), s32[]{:S(2)}) async-start(), calls=%async_computation.15 | async-start | bytes 6291456 | tf_op jit(solution)/shard_map/all_gather | solution.py:30
  686.1 85.7 %all-gather.23.cloned.1.call-start = ((), (), s32[]{:S(2)}) async-start(), calls=%async_computation.23 | async-start | bytes 6291456 | tf_op jit(solution)/shard_map/all_gather | solution.py:30
Sparse Core Ops, SparseCore 0:
  173.4 11.5 reduce-scatter.16
  208.9 11.5 reduce-scatter.20
  313.5 11.5 reduce-scatter.8
  349.2 11.5 reduce-scatter.12
  362.9 30.1 reduce-scatter.18
  395.2 29.0 reduce-scatter.22
  426.5 29.0 reduce-scatter.10
  457.7 29.0 reduce-scatter.14
  489.3 102.0 all-reduce.2
  592.8 30.0 all-gather.8
  624.4 30.0 all-gather.16
  655.9 30.1 all-gather.12
  687.6 30.1 all-gather.20
  719.2 11.2 all-gather.10
  731.8 12.3 all-gather.18
  745.6 12.3 all-gather.14
  759.4 12.3 all-gather.22
where the time goes:
time: 788 us; the launch traced here: 783 us
  waiting for transfers between devices  397 us (50%)
  matrix products  342 us (43%)
  other arithmetic  18.8 us (2%)
  between operations  14.2 us (2%)
  local copies, waits for them, and re-layouts  10.7 us (1%)
    reduce_scatter x4, waiting for transfers between devices, reduce_grad(): reduced = lax.psum_scatter(reduced, 'y', scatter_dimension=0, tiled=True)  126 us
    all_gather x4, waiting for transfers between devices, reduce_grad(): reduced = lax.all_gather(reduced, 'y', axis=0, tiled=True)  124 us
    psum x1, waiting for transfers between devices, reduce_grad(): reduced = lax.psum(reduced, 'z')  105 us
    dot_general x1, matrix products, device_step(): jnp.einsum('nd,fd->nf', g_loc, w_four, preferred_element_type=jnp.float32)  57.7 us
    dot_general x1, matrix products, device_step(): jnp.einsum('nd,fd->nf', d_h2, w_two, preferred_element_type=jnp.float32)  56.8 us
    dot_general x1, matrix products, device_step(): jnp.einsum('nf,nd->fd', h_one, d_h2, preferred_element_type=jnp.float32)  35.6 us
    dot_general x1, matrix products, device_step(): jnp.einsum('nf,nd->fd', h_three, g_loc, preferred_element_type=jnp.float32)  35.5 us
    dot_general x1, matrix products, device_step(): jnp.dot(h_one, w_two, preferred_element_type=jnp.float32)  33.7 us
  transfers between devices with their start and end apart: 17, of which 14 were waited for; matrix products, arithmetic and copies ran while one was open for 26% of the time, Pallas kernels for 0%

commit v1 on v0

v1 whole, which is shorter than its diff:
```python
import functools
import math

import jax
import jax.numpy as jnp
from jax import lax
from jax.experimental import pallas as pl
from jax.experimental.pallas import tpu as pltpu
from jax.sharding import PartitionSpec as P

MESH = pl.DeviceIdType.MESH
GELU_C = math.sqrt(2.0 / math.pi)
GELU_K = 0.044715

N = 8192
D = 512
F = 2048
FB = 256
NB = F // FB
T1 = 512
N1 = N // T1
T2 = 2048
N2 = N // T2
RC = 256
SLOTS = 4
OFFS = (0, 1, 4, 6, 8, 11, 13)
LAST_TRIP = 73 + OFFS[-1]

bf16 = jnp.bfloat16
f32 = jnp.float32


def dot(a, b):
    return jnp.dot(a, b, preferred_element_type=f32)


def dot_nt(a, b):
    return lax.dot_general(a, b, (((1,), (1,)), ((), ())), preferred_element_type=f32)


def gelu_half(a):
    sq = a * a
    t = jnp.tanh(a * (GELU_C + (GELU_C * GELU_K) * sq))
    s = 0.5 + 0.5 * t
    return sq, s, a * s


def gelu_and_grad(a):
    sq, s, h = gelu_half(a)
    g = s + (h * (1.0 - s)) * (2.0 * GELU_C + (6.0 * GELU_C * GELU_K) * sq)
    return h, g


def kernel(x_hbm, g_hbm, w1_hbm, w2_hbm, w3_hbm, w4_hbm, out, a1_hbm, da3_hbm,
           gn, gt, hn, ht, w1, w2, w3, w4, u0, u1, u2, u3, vv, xs,
           pacc, rx, sm, r1, r2, rs,
           ld_sem, x_sem, st_sem, ld2_sem, send_sem, recv_sem, loc_sem):
    z = lax.axis_index("z")
    y = lax.axis_index("y")
    c = lax.axis_index("xc")
    partner = (z, y, 1 - c)
    near_a = (lax.rem(z + c, 2), lax.rem(y + 1 - c, 2), c)
    near_b = (lax.rem(z + 1 - c, 2), lax.rem(y + c, 2), c)
    bit_a = y * (1 - c) + z * c
    bit_b = z * (1 - c) + y * c

    barrier = pltpu.get_barrier_semaphore()
    for dev in (partner, near_a, near_b):
        pl.semaphore_signal(barrier, inc=1, device_id=dev, device_id_type=MESH)

    def x_copy(i):
        slot = lax.rem(i, 4)
        return pltpu.make_async_copy(x_hbm.at[pl.ds(i * T1, T1)], xs.at[slot], x_sem.at[slot])

    loads = [
        pltpu.make_async_copy(w1_hbm, w1, ld_sem.at[0]),
        pltpu.make_async_copy(w2_hbm, w2, ld_sem.at[1]),
        pltpu.make_async_copy(g_hbm, gn, ld_sem.at[2]),
        pltpu.make_async_copy(w3_hbm, w3, ld_sem.at[3]),
        pltpu.make_async_copy(w4_hbm, w4, ld_sem.at[4]),
    ]
    loads[0].start()
    x_copy(0).start()
    x_copy(1).start()
    for ld in loads[1:]:
        ld.start()
    pl.semaphore_wait(barrier, 3)

    uu = (u0, u1, u2, u3)

    def a1_store(i, par, cc):
        return pltpu.make_async_copy(
            vv.at[2 * par + cc // 4, pl.ds((cc % 4) * T1, T1)],
            a1_hbm.at[cc, pl.ds(i * T1, T1)],
            st_sem.at[par],
        )

    def fwd_trip(i, par, wait_x):
        prev = lax.rem(i + N1 - 1, N1)
        if wait_x:
            x_copy(i).wait()
        xt = xs.at[lax.rem(i, 4)]
        acc = xs[lax.rem(i + 3, 4)].astype(f32)
        for cc in range(NB):
            a = dot(xt[...], w1[:, cc * FB:(cc + 1) * FB]).astype(bf16)
            vv[2 * par + cc // 4, (cc % 4) * T1:(cc % 4 + 1) * T1, :] = a
            _, _, h = gelu_half(a.astype(f32))
            uu[2 * par + cc // 4][(cc % 4) * T1:(cc % 4 + 1) * T1, :] = h.astype(bf16)
        res = None
        for cc in range(NB):
            hb = uu[2 * (1 - par) + cc // 4][(cc % 4) * T1:(cc % 4 + 1) * T1, :]
            term = dot(hb, w2[cc * FB:(cc + 1) * FB, :])
            res = term if res is None else res + term
        h2 = (res + acc).astype(bf16)
        hn[pl.ds(pl.multiple_of(prev * T1, T1), T1), :] = h2
        ht[prev // 4, :, pl.ds(pl.multiple_of(lax.rem(prev, 4) * T1, T1), T1)] = h2.T
        gt[i // 4, :, pl.ds(pl.multiple_of(lax.rem(i, 4) * T1, T1), T1)] = gn[pl.ds(pl.multiple_of(i * T1, T1), T1), :].T

    for ld in loads[:3]:
        ld.wait()

    def fwd_pair(k, carry):
        for par in (0, 1):
            i = 2 * k + par

            @pl.when(i >= 2)
            def _():
                for cc in range(NB):
                    a1_store(i - 2, par, cc).wait()

            @pl.when(i + 2 < N1)
            def _():
                x_copy(i + 2).start()

            x_copy(i).wait()
            fwd_trip(i, par, False)
            for cc in range(NB):
                a1_store(i, par, cc).start()
        return carry

    lax.fori_loop(0, N1 // 2, fwd_pair, 0)
    res = None
    for cc in range(NB):
        hb = uu[2 + cc // 4][(cc % 4) * T1:(cc % 4 + 1) * T1, :]
        term = dot(hb, w2[cc * FB:(cc + 1) * FB, :])
        res = term if res is None else res + term
    h2 = (res + xs[(N1 - 1) % 4].astype(f32)).astype(bf16)
    hn[N - T1:N, :] = h2
    ht[N2 - 1, :, T2 - T1:T2] = h2.T
    for par in (0, 1):
        for cc in range(NB):
            a1_store(N1 - 2 + par, par, cc).wait()
    for ld in loads[3:]:
        ld.wait()

    def half(b):
        return pl.ds(pl.multiple_of(b * (D // 2), D // 2), D // 2)

    def quarter(a, b):
        return pl.ds(pl.multiple_of(a * (D // 2) + b * (D // 4), D // 4), D // 4)

    def remote(src, dst, slot, step, dev):
        return pltpu.make_async_remote_copy(
            src_ref=src, dst_ref=dst, send_sem=send_sem.at[slot, step], recv_sem=recv_sem.at[slot, step],
            device_id=dev, device_id_type=MESH)

    def cp_pair(p, s):
        return remote(pacc.at[lax.rem(p, 2), 1 - c], rx.at[s], s, 0, partner)

    def cp_s1(p, s):
        return remote(sm.at[s, half(1 - bit_a)], r1.at[s], s, 1, near_a)

    def cp_s2(p, s):
        return remote(sm.at[s, quarter(bit_a, 1 - bit_b)], r2.at[s], s, 2, near_b)

    def cp_s3(p, s):
        rows = quarter(bit_a, bit_b)
        return remote(rs.at[s, rows], rs.at[s, rows], s, 3, near_b)

    def cp_s4(p, s):
        rows = half(bit_a)
        return remote(rs.at[s, rows], rs.at[s, rows], s, 4, near_a)

    def cp_s5(p, s):
        return remote(rs.at[s], out.at[p, c], s, 5, partner)

    def cp_loc(p, s):
        return pltpu.make_async_copy(rs.at[s], out.at[p, c], loc_sem.at[s])

    def h_pair_send(p, s):
        cp_pair(p, s).start()

    def h_s1(p, s):
        cp_pair(p, s).wait()
        sm[s] = pacc[lax.rem(p, 2), c] + rx[s]
        cp_s1(p, s).start()

    def h_s2(p, s):
        cp_s1(p, s).wait()
        rows = half(bit_a)
        sm[s, rows] = sm[s, rows] + r1[s]
        cp_s2(p, s).start()

    def h_s3(p, s):
        cp_s2(p, s).wait()
        rows = quarter(bit_a, bit_b)
        rs[s, rows] = (sm[s, rows] + r2[s]) * 0.125
        cp_s3(p, s).start()

    def h_s4(p, s):
        cp_s3(p, s).wait()
        cp_s4(p, s).start()

    def h_s5(p, s):
        cp_s4(p, s).wait()
        cp_s5(p, s).start()
        cp_loc(p, s).start()

    def h_end(p, s):
        cp_s5(p, s).wait()
        cp_loc(p, s).wait()

    stages = (h_pair_send, h_s1, h_s2, h_s3, h_s4, h_s5, h_end)

    def comm(f):
        for order in (0, 6, 5, 4, 3, 2, 1):
            q = f + (40 - 5 - OFFS[order])
            k = q // 4 - 10
            ok = jnp.logical_and(
                lax.rem(q, 4) == 0,
                jnp.logical_or(jnp.logical_and(k >= 0, k < NB), jnp.logical_and(k >= NB + 2, k < 2 * NB + 2)))

            @pl.when(ok)
            def _():
                p = jnp.where(k >= NB + 2, k - 2, k)
                stages[order](p, lax.rem(p, SLOTS))

    def accumulate(par, idx, first, value):
        old = pacc[par, idx]
        if first is not None:
            old = jnp.where(first, 0.0, old)
        pacc[par, idx] = old + value

    def b_part(lhs0, lhs1, tb, par, pb, first):
        accumulate(par, 0, first, dot(lhs0[tb], uu[pb][...]))
        accumulate(par, 1, first, dot(lhs1[tb], uu[2 + pb][...]))

    def da3_store(f, par):
        return pltpu.make_async_copy(
            uu[2 + par], da3_hbm.at[f // N2, pl.ds(lax.rem(f, N2) * T2, T2)], st_sem.at[par])

    def l2_trip(f, par):
        t = lax.rem(f, N2)
        j = f // N2
        col = pl.ds(pl.multiple_of(j * FB, FB), FB)
        before = f + N2 - 1
        tb = lax.rem(before, N2)
        pp = lax.rem(before // N2 + 1, 2)
        w3j = w3[:, col]
        w4j = w4[col, :]
        for rc in range(T2 // RC):
            rows = pl.ds(pl.multiple_of(t * T2 + rc * RC, RC), RC)
            a = dot(hn[rows, :], w3j).astype(bf16).astype(f32)
            d = dot_nt(gn[rows, :], w4j)
            h, g = gelu_and_grad(a)
            uu[par][rc * RC:(rc + 1) * RC, :] = h.astype(bf16)
            uu[2 + par][rc * RC:(rc + 1) * RC, :] = (d * g).astype(bf16)
        b_part(gt, ht, tb, pp, 1 - par, None if par == 0 else tb == 0)

    def l2_pair(k, carry):
        for par in (0, 1):
            f = 2 * k + par
            comm(f)

            @pl.when(f >= 2)
            def _():
                da3_store(f - 2, par).wait()

            l2_trip(f, par)
            da3_store(f, par).start()
        return carry

    lax.fori_loop(0, NB * N2 // 2, l2_pair, 0)
    b_part(gt, ht, N2 - 1, (NB - 1) % 2, 1, None)
    for par in (0, 1):
        da3_store(NB * N2 - 2 + par, par).wait()

    def da3_load(i, par, cc):
        return pltpu.make_async_copy(
            da3_hbm.at[cc, pl.ds(i * T1, T1)],
            vv.at[2 * par + cc // 4, pl.ds((cc % 4) * T1, T1)],
            ld2_sem.at[par],
        )

    def da3_start(i, par):
        for cc in range(NB):
            da3_load(i, par, cc).start()
        x_copy(i).start()

    da3_start(0, 0)
    da3_start(1, 1)

    def dh2_pair(k, carry):
        comm(NB * N2 + k)
        for par in (0, 1):
            i = 2 * k + par
            for cc in range(NB):
                da3_load(i, par, cc).wait()
            x_copy(i).wait()
            rows = pl.ds(pl.multiple_of(i * T1, T1), T1)
            lanes = pl.ds(pl.multiple_of(lax.rem(i, 4) * T1, T1), T1)
            res = None
            for cc in range(NB):
                term = dot_nt(vv[2 * par + cc // 4, (cc % 4) * T1:(cc % 4 + 1) * T1, :], w3[:, cc * FB:(cc + 1) * FB])
                res = term if res is None else res + term
            dh2 = (res + gn[rows, :].astype(f32)).astype(bf16)
            hn[rows, :] = dh2
            ht[i // 4, :, lanes] = dh2.T
            gt[i // 4, :, lanes] = xs[lax.rem(i, 4)].T

            @pl.when(i + 2 < N1)
            def _():
                da3_start(i + 2, par)
        return carry

    lax.fori_loop(0, N1 // 2, dh2_pair, 0)

    base = NB * N2 + N1 // 2

    def a1_load(f):
        slot = lax.rem(f, 4)
        return pltpu.make_async_copy(
            a1_hbm.at[f // N2, pl.ds(lax.rem(f, N2) * T2, T2)], vv.at[slot], x_sem.at[slot])

    for f0 in range(3):
        a1_load(f0).start()

    def l1_trip(f, par):
        t = lax.rem(f, N2)
        j = f // N2
        col = pl.ds(pl.multiple_of(j * FB, FB), FB)
        before = f + N2 - 1
        tb = lax.rem(before, N2)
        pp = lax.rem(before // N2 + 1, 2)
        slot = lax.rem(f, 4)
        w2j = w2[col, :]
        for rc in range(T2 // RC):
            rows = pl.ds(pl.multiple_of(t * T2 + rc * RC, RC), RC)
            a = vv[slot, rc * RC:(rc + 1) * RC, :].astype(f32)
            d = dot_nt(hn[rows, :], w2j)
            h, g = gelu_and_grad(a)
            uu[par][rc * RC:(rc + 1) * RC, :] = h.astype(bf16)
            uu[2 + par][rc * RC:(rc + 1) * RC, :] = (d * g).astype(bf16)
        b_part(ht, gt, tb, pp, 1 - par, None if par == 0 else tb == 0)

    def l1_pair(k, carry):
        for par in (0, 1):
            f = 2 * k + par
            comm(base + f)

            @pl.when(f + 3 < NB * N2)
            def _():
                a1_load(f + 3).start()

            a1_load(f).wait()
            l1_trip(f, par)
        return carry

    lax.fori_loop(0, NB * N2 // 2, l1_pair, 0)
    comm(base + NB * N2)
    b_part(ht, gt, N2 - 1, (NB - 1) % 2, 1, None)

    def tail(k, carry):
        comm(base + NB * N2 + 1 + k)
        return carry

    lax.fori_loop(0, LAST_TRIP - base - NB * N2, tail, 0)


def finish_kernel(p2, p1, o1, o2, o3, o4):
    o1[...] = p1[0, 1]
    o2[...] = p1[0, 0].T
    o3[...] = p2[0, 1]
    o4[...] = p2[0, 0].T


def device_step(x_loc, g_loc, w_one, w_two, w_three, w_four):
    any_spec = pl.BlockSpec(memory_space=pl.ANY)
    sums, _, _ = pl.pallas_call(
        kernel,
        name="grads",
        out_shape=(
            jax.ShapeDtypeStruct((2 * NB, 2, D, FB), f32),
            jax.ShapeDtypeStruct((NB, N, FB), bf16),
            jax.ShapeDtypeStruct((NB, N, FB), bf16),
        ),
        in_specs=[any_spec] * 6,
        out_specs=(any_spec,) * 3,
        scratch_shapes=[
            pltpu.VMEM((N, D), bf16),
            pltpu.VMEM((N2, D, T2), bf16),
            pltpu.VMEM((N, D), bf16),
            pltpu.VMEM((N2, D, T2), bf16),
            pltpu.VMEM((D, F), bf16),
            pltpu.VMEM((F, D), bf16),
            pltpu.VMEM((D, F), bf16),
            pltpu.VMEM((F, D), bf16),
            pltpu.VMEM((T2, FB), bf16),
            pltpu.VMEM((T2, FB), bf16),
            pltpu.VMEM((T2, FB), bf16),
            pltpu.VMEM((T2, FB), bf16),
            pltpu.VMEM((4, T2, FB), bf16),
            pltpu.VMEM((4, T1, D), bf16),
            pltpu.VMEM((2, 2, D, FB), f32),
            pltpu.VMEM((SLOTS, D, FB), f32),
            pltpu.VMEM((SLOTS, D, FB), f32),
            pltpu.VMEM((SLOTS, D // 2, FB), f32),
            pltpu.VMEM((SLOTS, D // 4, FB), f32),
            pltpu.VMEM((SLOTS, D, FB), f32),
            pltpu.SemaphoreType.DMA((5,)),
            pltpu.SemaphoreType.DMA((4,)),
            pltpu.SemaphoreType.DMA((2,)),
            pltpu.SemaphoreType.DMA((2,)),
            pltpu.SemaphoreType.DMA((SLOTS, 6)),
            pltpu.SemaphoreType.DMA((SLOTS, 6)),
            pltpu.SemaphoreType.DMA((SLOTS,)),
        ],
        compiler_params=pltpu.CompilerParams(
            collective_id=0, has_side_effects=True, vmem_limit_bytes=67000000),
        cost_estimate=pl.CostEstimate(flops=20 * N * D * F, bytes_accessed=200 << 20, transcendentals=3 * N * F),
    )(x_loc, g_loc, w_one, w_two, w_three, w_four)
    wide = jax.ShapeDtypeStruct((D, F), f32)
    tall = jax.ShapeDtypeStruct((F, D), f32)
    wide_spec = pl.BlockSpec((D, FB), lambda j: (0, j))
    tall_spec = pl.BlockSpec((FB, D), lambda j: (j, 0))
    return pl.pallas_call(
        finish_kernel,
        name="finish",
        grid=(NB,),
        out_shape=(wide, tall, wide, tall),
        in_specs=[
            pl.BlockSpec((1, 2, D, FB), lambda j: (j, 0, 0, 0)),
            pl.BlockSpec((1, 2, D, FB), lambda j: (j + NB, 0, 0, 0)),
        ],
        out_specs=(wide_spec, tall_spec, wide_spec, tall_spec),
    )(sums, sums)


def solution(mesh):
    batch_spec = P(("z", "y", "xc"), None)
    whole_spec = P(None, None)
    return jax.shard_map(
        device_step,
        mesh=mesh,
        in_specs=(batch_spec, batch_spec, whole_spec, whole_spec, whole_spec, whole_spec),
        out_specs=(whole_spec, whole_spec, whole_spec, whole_spec),
        check_vma=False,
    )
```

time: 788 us -> 309 us (0.39)
  waiting for transfers between devices: 397 us -> 0 us
  matrix products: 342 us -> 0 us
  Pallas kernels: 0 us -> 308 us
  other arithmetic: 18.8 us -> 0 us
  between operations: 14.2 us -> 0.64 us
  local copies, waits for them, and re-layouts: 10.7 us -> 0 us
    dot_general x10 -> x0, matrix products: 342 us -> none  [the longest x1 57.7 us: device_step(): jnp.einsum('nd,fd->nf', g_loc, w_four, preferred_element_type=jnp.float32)]
    pallas_call x0 -> x2, Pallas kernels: none -> 308 us  [the longest x1 294 us: device_step(): pl.pallas_call(kernel, name='grads', out_shape=(jax.ShapeDtypeStruct((2 *...]
    all_gather x8 -> x0, waiting for transfers between devices: 153 us -> none  [the longest x4 124 us: reduce_grad(): reduced = lax.all_gather(reduced, 'y', axis=0, tiled=True)]
    reduce_scatter x8 -> x0, waiting for transfers between devices: 136 us -> none  [the longest x4 126 us: reduce_grad(): reduced = lax.psum_scatter(reduced, 'y', scatter_dimension=0, tiled=True)]
    psum x1 -> x0, waiting for transfers between devices: 105 us -> none  [reduce_grad(): reduced = lax.psum(reduced, 'z')]
    div x4 -> x0, other arithmetic: 18.8 us -> none  [reduce_grad(): return reduced / n_dev]
    unnamed x8 -> x0, local copies, waits for them, and re-layouts: 10.7 us -> none
  transfers between devices with their start and end apart: 17 -> 0, of which waited for: 14 -> 0; matrix products, arithmetic and copies ran while one was open for 26% -> 0% of each run, Pallas kernels for 0% -> 0%
where the time goes in v1:
time: 309 us
  Pallas kernels  308 us (100%)
    pallas_call x1, Pallas kernels, device_step(): pl.pallas_call(kernel, name='grads', out_shape=(jax.ShapeDtypeStruct((2 *...  294 us
    pallas_call x1, Pallas kernels, device_step(): pl.pallas_call(finish_kernel, name='finish', grid=(NB,), out_shape=(wide,...  13.7 us

profile of v1, /device:TPU:0, one launch (start us, length us, event | category | flops | bytes accessed | tf_op | source)
XLA Modules:
  0.0 308.7 jit_solution(12024265500481138540)
XLA Ops:
  0.6 294.3 %grads.1 = (f32[16,2,512,256]{3,2,1,0:T(8,128)}, bf16[8,8192,256]{2,1,0:T(8,128)(2,1)}, bf16[8,8192,256]{2,1,0:T(8,128)(2,1)}) custom-call(bf16[8192,512]{1,0:T(8,128)(2,1)} %x_hbm.1, bf16[8192,512]{1,0:T(8,128)(2,1)} %g_hbm.1, bf16[512,2048]{1,0:T(8,128)(2,1)} %w1_hbm.1, bf16[2048,512]{1,0:T(8,128)(2,1)} %w2_hbm.1, bf16[512,2048]{1,0:T(8,128)(2,1)} %w3_hbm.1, ...), custom_call_target="tpu_custom_call" | custom-call | flops 171798691840 | bytes 209715200 | tf_op jit(solution)/shard_map/grads/pallas_call | solution.py:389
  294.9 13.7 %finish.1 = (f32[512,2048]{1,0:T(8,128)}, f32[2048,512]{1,0:T(8,128)}, f32[512,2048]{1,0:T(8,128)}, f32[2048,512]{1,0:T(8,128)}) custom-call(f32[16,2,512,256]{3,2,1,0:T(8,128)} %get-tuple-element.5.p2.p1, f32[16,2,512,256]{3,2,1,0:T(8,128)} %get-tuple-element.5.p2.p1), custom_call_target="tpu_custom_call" | custom-call | tf_op jit(solution)/shard_map/finish/pallas_call | solution.py:436

commit v2 on v1

--- a/solution.py
+++ b/solution.py
@@ -23,7 +23,8 @@
 N2 = N // T2
 RC = 256
 SLOTS = 4
-OFFS = (0, 1, 4, 6, 8, 11, 13)
+SEMS = 8
+OFFS = (0, 2, 6, 9, 12, 16, 18)
 LAST_TRIP = 73 + OFFS[-1]
 
 bf16 = jnp.bfloat16
@@ -159,66 +160,74 @@
     def quarter(a, b):
         return pl.ds(pl.multiple_of(a * (D // 2) + b * (D // 4), D // 4), D // 4)
 
-    def remote(src, dst, slot, step, dev):
+    def remote(src, dst, p, step, dev):
+        e = lax.rem(p, SEMS)
         return pltpu.make_async_remote_copy(
-            src_ref=src, dst_ref=dst, send_sem=send_sem.at[slot, step], recv_sem=recv_sem.at[slot, step],
+            src_ref=src, dst_ref=dst, send_sem=send_sem.at[e, step], recv_sem=recv_sem.at[e, step],
             device_id=dev, device_id_type=MESH)
 
-    def cp_pair(p, s):
-        return remote(pacc.at[lax.rem(p, 2), 1 - c], rx.at[s], s, 0, partner)
-
-    def cp_s1(p, s):
-        return remote(sm.at[s, half(1 - bit_a)], r1.at[s], s, 1, near_a)
-
-    def cp_s2(p, s):
-        return remote(sm.at[s, quarter(bit_a, 1 - bit_b)], r2.at[s], s, 2, near_b)
-
-    def cp_s3(p, s):
+    def cp_pair(p):
+        e = lax.rem(p, 2)
+        return remote(pacc.at[e, 1 - c], rx.at[e], p, 0, partner)
+
+    def cp_s1(p):
+        e = lax.rem(p, 2)
+        return remote(sm.at[e, half(1 - bit_a)], r1.at[e], p, 1, near_a)
+
+    def cp_s2(p):
+        e = lax.rem(p, 2)
+        return remote(sm.at[e, quarter(bit_a, 1 - bit_b)], r2.at[e], p, 2, near_b)
+
+    def cp_s3(p):
+        part = rs.at[lax.rem(p, SLOTS), quarter(bit_a, bit_b)]
+        return remote(part, part, p, 3, near_b)
+
+    def cp_s4(p):
+        part = rs.at[lax.rem(p, SLOTS), half(bit_a)]
+        return remote(part, part, p, 4, near_a)
+
+    def cp_s5(p):
+        return remote(rs.at[lax.rem(p, SLOTS)], out.at[p, c], p, 5, partner)
+
+    def cp_loc(p):
+        e = lax.rem(p, SLOTS)
+        return pltpu.make_async_copy(rs.at[e], out.at[p, c], loc_sem.at[e])
+
+    def h_pair_send(p):
+        cp_pair(p).start()
+
+    def h_s1(p):
+        cp_pair(p).wait()
+        e = lax.rem(p, 2)
+        sm[e] = pacc[e, c] + rx[e]
+        cp_s1(p).start()
+
+    def h_s2(p):
+        cp_s1(p).wait()
+        e = lax.rem(p, 2)
+        rows = half(bit_a)
+        sm[e, rows] = sm[e, rows] + r1[e]
+        cp_s2(p).start()
+
+    def h_s3(p):
+        cp_s2(p).wait()
+        e = lax.rem(p, 2)
         rows = quarter(bit_a, bit_b)
-        return remote(rs.at[s, rows], rs.at[s, rows], s, 3, near_b)
-
-    def cp_s4(p, s):
-        rows = half(bit_a)
-        return remote(rs.at[s, rows], rs.at[s, rows], s, 4, near_a)
-
-    def cp_s5(p, s):
-        return remote(rs.at[s], out.at[p, c], s, 5, partner)
-
-    def cp_loc(p, s):
-        return pltpu.make_async_copy(rs.at[s], out.at[p, c], loc_sem.at[s])
-
-    def h_pair_send(p, s):
-        cp_pair(p, s).start()
-
-    def h_s1(p, s):
-        cp_pair(p, s).wait()
-        sm[s] = pacc[lax.rem(p, 2), c] + rx[s]
-        cp_s1(p, s).start()
-
-    def h_s2(p, s):
-        cp_s1(p, s).wait()
-        rows = half(bit_a)
-        sm[s, rows] = sm[s, rows] + r1[s]
-        cp_s2(p, s).start()
-
-    def h_s3(p, s):
-        cp_s2(p, s).wait()
-        rows = quarter(bit_a, bit_b)
-        rs[s, rows] = (sm[s, rows] + r2[s]) * 0.125
-        cp_s3(p, s).start()
-
-    def h_s4(p, s):
-        cp_s3(p, s).wait()
-        cp_s4(p, s).start()
-
-    def h_s5(p, s):
-        cp_s4(p, s).wait()
-        cp_s5(p, s).start()
-        cp_loc(p, s).start()
-
-    def h_end(p, s):
-        cp_s5(p, s).wait()
-        cp_loc(p, s).wait()
+        rs[lax.rem(p, SLOTS), rows] = (sm[e, rows] + r2[e]) * 0.125
+        cp_s3(p).start()
+
+    def h_s4(p):
+        cp_s3(p).wait()
+        cp_s4(p).start()
+
+    def h_s5(p):
+        cp_s4(p).wait()
+        cp_s5(p).start()
+        cp_loc(p).start()
+
+    def h_end(p):
+        cp_s5(p).wait()
+        cp_loc(p).wait()
 
     stages = (h_pair_send, h_s1, h_s2, h_s3, h_s4, h_s5, h_end)
 
@@ -232,8 +241,7 @@
 
             @pl.when(ok)
             def _():
-                p = jnp.where(k >= NB + 2, k - 2, k)
-                stages[order](p, lax.rem(p, SLOTS))
+                stages[order](k - 2 * (k // (NB + 2)))
 
     def accumulate(par, idx, first, value):
         old = pacc[par, idx]
@@ -377,11 +385,18 @@
     lax.fori_loop(0, LAST_TRIP - base - NB * N2, tail, 0)
 
 
-def finish_kernel(p2, p1, o1, o2, o3, o4):
-    o1[...] = p1[0, 1]
-    o2[...] = p1[0, 0].T
-    o3[...] = p2[0, 1]
-    o4[...] = p2[0, 0].T
+def finish_kernel(piece, o1, o2, o3, o4):
+    p = pl.program_id(0)
+
+    @pl.when(p < NB)
+    def _():
+        o3[...] = piece[0, 1]
+        o4[...] = piece[0, 0].T
+
+    @pl.when(p >= NB)
+    def _():
+        o1[...] = piece[0, 1]
+        o2[...] = piece[0, 0].T
 
 
 def device_step(x_loc, g_loc, w_one, w_two, w_three, w_four):
@@ -412,17 +427,17 @@
             pltpu.VMEM((4, T2, FB), bf16),
             pltpu.VMEM((4, T1, D), bf16),
             pltpu.VMEM((2, 2, D, FB), f32),
-            pltpu.VMEM((SLOTS, D, FB), f32),
-            pltpu.VMEM((SLOTS, D, FB), f32),
-            pltpu.VMEM((SLOTS, D // 2, FB), f32),
-            pltpu.VMEM((SLOTS, D // 4, FB), f32),
+            pltpu.VMEM((2, D, FB), f32),
+            pltpu.VMEM((2, D, FB), f32),
+            pltpu.VMEM((2, D // 2, FB), f32),
+            pltpu.VMEM((2, D // 4, FB), f32),
             pltpu.VMEM((SLOTS, D, FB), f32),
             pltpu.SemaphoreType.DMA((5,)),
             pltpu.SemaphoreType.DMA((4,)),
             pltpu.SemaphoreType.DMA((2,)),
             pltpu.SemaphoreType.DMA((2,)),
-            pltpu.SemaphoreType.DMA((SLOTS, 6)),
-            pltpu.SemaphoreType.DMA((SLOTS, 6)),
+            pltpu.SemaphoreType.DMA((SEMS, 6)),
+            pltpu.SemaphoreType.DMA((SEMS, 6)),
             pltpu.SemaphoreType.DMA((SLOTS,)),
         ],
         compiler_params=pltpu.CompilerParams(
@@ -431,19 +446,19 @@
     )(x_loc, g_loc, w_one, w_two, w_three, w_four)
     wide = jax.ShapeDtypeStruct((D, F), f32)
     tall = jax.ShapeDtypeStruct((F, D), f32)
-    wide_spec = pl.BlockSpec((D, FB), lambda j: (0, j))
-    tall_spec = pl.BlockSpec((FB, D), lambda j: (j, 0))
     return pl.pallas_call(
         finish_kernel,
         name="finish",
-        grid=(NB,),
+        grid=(2 * NB,),
         out_shape=(wide, tall, wide, tall),
-        in_specs=[
-            pl.BlockSpec((1, 2, D, FB), lambda j: (j, 0, 0, 0)),
-            pl.BlockSpec((1, 2, D, FB), lambda j: (j + NB, 0, 0, 0)),
-        ],
-        out_specs=(wide_spec, tall_spec, wide_spec, tall_spec),
-    )(sums, sums)
+        in_specs=[pl.BlockSpec((1, 2, D, FB), lambda p: (p, 0, 0, 0))],
+        out_specs=(
+            pl.BlockSpec((D, FB), lambda p: (0, jnp.maximum(p - NB, 0))),
+            pl.BlockSpec((FB, D), lambda p: (jnp.maximum(p - NB, 0), 0)),
+            pl.BlockSpec((D, FB), lambda p: (0, jnp.minimum(p, NB - 1))),
+            pl.BlockSpec((FB, D), lambda p: (jnp.minimum(p, NB - 1), 0)),
+        ),
+    )(sums)
 
 
 def solution(mesh):

time: 309 us -> 319 us (1.032)
  Pallas kernels: 308 us -> 318 us
    pallas_call x1, Pallas kernels: 294 us -> 300 us  [device_step(): pl.pallas_call(kernel, name='grads', out_shape=(jax.ShapeDtypeStruct((2 *...]
    pallas_call x1, Pallas kernels: 13.7 us -> 18.3 us  [device_step(): pl.pallas_call(finish_kernel, name='finish', grid=(2 * NB,), out_shape=(w...]
where the time goes in v2:
time: 319 us
  Pallas kernels  318 us (100%)
    pallas_call x1, Pallas kernels, device_step(): pl.pallas_call(kernel, name='grads', out_shape=(jax.ShapeDtypeStruct((2 *...  300 us
    pallas_call x1, Pallas kernels, device_step(): pl.pallas_call(finish_kernel, name='finish', grid=(2 * NB,), out_shape=(w...  18.3 us

profile of v2, /device:TPU:0, one launch (start us, length us, event | category | flops | bytes accessed | tf_op | source)
XLA Modules:
  0.0 318.7 jit_solution(11196464476976855260)
XLA Ops:
  0.6 299.8 %grads.1 = (f32[16,2,512,256]{3,2,1,0:T(8,128)}, bf16[8,8192,256]{2,1,0:T(8,128)(2,1)}, bf16[8,8192,256]{2,1,0:T(8,128)(2,1)}) custom-call(bf16[8192,512]{1,0:T(8,128)(2,1)} %x_hbm.1, bf16[8192,512]{1,0:T(8,128)(2,1)} %g_hbm.1, bf16[512,2048]{1,0:T(8,128)(2,1)} %w1_hbm.1, bf16[2048,512]{1,0:T(8,128)(2,1)} %w2_hbm.1, bf16[512,2048]{1,0:T(8,128)(2,1)} %w3_hbm.1, ...), custom_call_target="tpu_custom_call" | custom-call | flops 171798691840 | bytes 209715200 | tf_op jit(solution)/shard_map/grads/pallas_call | solution.py:404
  300.4 18.3 %finish.1 = (f32[512,2048]{1,0:T(8,128)}, f32[2048,512]{1,0:T(8,128)}, f32[512,2048]{1,0:T(8,128)}, f32[2048,512]{1,0:T(8,128)}) custom-call(f32[16,2,512,256]{3,2,1,0:T(8,128)} %get-tuple-element.5.piece), custom_call_target="tpu_custom_call" | custom-call | tf_op jit(solution)/shard_map/finish/pallas_call | solution.py:449

commit v3 on v2

--- a/solution.py
+++ b/solution.py
@@ -19,9 +19,14 @@
 NB = F // FB
 T1 = 512
 N1 = N // T1
+RH = T1 // 2
 T2 = 2048
 N2 = N // T2
-RC = 256
+RC2 = 128
+RC1 = 256
+KU = 256
+RA = 128
+UNITS = 2 * (T2 // KU)
 SLOTS = 4
 SEMS = 8
 OFFS = (0, 2, 6, 9, 12, 16, 18)
@@ -33,10 +38,6 @@
 
 def dot(a, b):
     return jnp.dot(a, b, preferred_element_type=f32)
-
-
-def dot_nt(a, b):
-    return lax.dot_general(a, b, (((1,), (1,)), ((), ())), preferred_element_type=f32)
 
 
 def gelu_half(a):
@@ -53,7 +54,7 @@
 
 
 def kernel(x_hbm, g_hbm, w1_hbm, w2_hbm, w3_hbm, w4_hbm, out, a1_hbm, da3_hbm,
-           gn, gt, hn, ht, w1, w2, w3, w4, u0, u1, u2, u3, vv, xs,
+           gn, gt, hn, ht, w1, w2, w3, w4, w4t, u0, u1, u2, u3, vv, xs,
            pacc, rx, sm, r1, r2, rs,
            ld_sem, x_sem, st_sem, ld2_sem, send_sem, recv_sem, loc_sem):
     z = lax.axis_index("z")
@@ -96,33 +97,59 @@
             st_sem.at[par],
         )
 
-    def fwd_trip(i, par, wait_x):
-        prev = lax.rem(i + N1 - 1, N1)
-        if wait_x:
-            x_copy(i).wait()
+    def h1_part(par, m, cc):
+        return uu[2 * par + cc // 4][(cc % 4) * T1 + m * RH:(cc % 4) * T1 + (m + 1) * RH, :]
+
+    def h2_unit(par, m, cc, total):
+        term = dot(h1_part(par, m, cc), w2[cc * FB:(cc + 1) * FB, :])
+        return term if total is None else total + term
+
+    def h2_store(i, m, total, x_rows):
+        h2 = (total + x_rows.astype(f32)).astype(bf16)
+        hn[pl.ds(pl.multiple_of(i * T1 + m * RH, RH), RH), :] = h2
+        ht[i, :, m * RH:(m + 1) * RH] = h2.T
+
+    def fwd_trip(i, par, with_a, with_b):
         xt = xs.at[lax.rem(i, 4)]
-        acc = xs[lax.rem(i + 3, 4)].astype(f32)
-        for cc in range(NB):
-            a = dot(xt[...], w1[:, cc * FB:(cc + 1) * FB]).astype(bf16)
-            vv[2 * par + cc // 4, (cc % 4) * T1:(cc % 4 + 1) * T1, :] = a
-            _, _, h = gelu_half(a.astype(f32))
-            uu[2 * par + cc // 4][(cc % 4) * T1:(cc % 4 + 1) * T1, :] = h.astype(bf16)
-        res = None
-        for cc in range(NB):
-            hb = uu[2 * (1 - par) + cc // 4][(cc % 4) * T1:(cc % 4 + 1) * T1, :]
-            term = dot(hb, w2[cc * FB:(cc + 1) * FB, :])
-            res = term if res is None else res + term
-        h2 = (res + acc).astype(bf16)
-        hn[pl.ds(pl.multiple_of(prev * T1, T1), T1), :] = h2
-        ht[prev // 4, :, pl.ds(pl.multiple_of(lax.rem(prev, 4) * T1, T1), T1)] = h2.T
-        gt[i // 4, :, pl.ds(pl.multiple_of(lax.rem(i, 4) * T1, T1), T1)] = gn[pl.ds(pl.multiple_of(i * T1, T1), T1), :].T
-
-    for ld in loads[:3]:
+        xp = xs.at[lax.rem(i + 3, 4)]
+        total = None
+        chunks = NB * (T1 // RA)
+        for n in range(chunks):
+            if with_a:
+                cc, r = n // (T1 // RA), n % (T1 // RA)
+                a = dot(xt[r * RA:(r + 1) * RA, :], w1[:, cc * FB:(cc + 1) * FB]).astype(bf16)
+                lo = (cc % 4) * T1 + r * RA
+                vv[2 * par + cc // 4, lo:lo + RA, :] = a
+                _, _, h = gelu_half(a.astype(f32))
+                uu[2 * par + cc // 4][lo:lo + RA, :] = h.astype(bf16)
+            if with_b:
+                for n2 in range(n * 2 * NB // chunks, (n + 1) * 2 * NB // chunks):
+                    m, cc = n2 // NB, n2 % NB
+                    total = h2_unit(1 - par, m, cc, total if cc else None)
+                    if cc == NB - 1:
+                        h2_store(i - 1, m, total, xp[m * RH:(m + 1) * RH, :])
+        if with_a:
+            rows = pl.ds(pl.multiple_of(i * T1, T1), T1)
+            gt[i] = gn[rows, :].T
+
+    def fwd_tail_transposes(i):
+        lanes = pl.ds(pl.multiple_of(i * (F // N1), F // N1), F // N1)
+        w4t[:, lanes] = w4[lanes, :].T
+
+    loads[0].wait()
+    x_copy(0).wait()
+    x_copy(2).start()
+    loads[2].wait()
+    fwd_trip(0, 0, True, False)
+    for cc in range(NB):
+        a1_store(0, 0, cc).start()
+    for ld in (loads[1], loads[3], loads[4]):
         ld.wait()
+    fwd_tail_transposes(0)
 
     def fwd_pair(k, carry):
-        for par in (0, 1):
-            i = 2 * k + par
+        for par in (1, 0):
+            i = 2 * k + 2 - par
 
             @pl.when(i >= 2)
             def _():
@@ -134,25 +161,24 @@
                 x_copy(i + 2).start()
 
             x_copy(i).wait()
-            fwd_trip(i, par, False)
+            fwd_trip(i, par, True, True)
+            fwd_tail_transposes(i)
             for cc in range(NB):
                 a1_store(i, par, cc).start()
         return carry
 
-    lax.fori_loop(0, N1 // 2, fwd_pair, 0)
-    res = None
+    lax.fori_loop(0, N1 // 2 - 1, fwd_pair, 0)
     for cc in range(NB):
-        hb = uu[2 + cc // 4][(cc % 4) * T1:(cc % 4 + 1) * T1, :]
-        term = dot(hb, w2[cc * FB:(cc + 1) * FB, :])
-        res = term if res is None else res + term
-    h2 = (res + xs[(N1 - 1) % 4].astype(f32)).astype(bf16)
-    hn[N - T1:N, :] = h2
-    ht[N2 - 1, :, T2 - T1:T2] = h2.T
+        a1_store(N1 - 3, 1, cc).wait()
+    x_copy(N1 - 1).wait()
+    fwd_trip(N1 - 1, 1, True, True)
+    fwd_tail_transposes(N1 - 1)
+    for cc in range(NB):
+        a1_store(N1 - 1, 1, cc).start()
+    fwd_trip(N1, 0, False, True)
     for par in (0, 1):
         for cc in range(NB):
             a1_store(N1 - 2 + par, par, cc).wait()
-    for ld in loads[3:]:
-        ld.wait()
 
     def half(b):
         return pl.ds(pl.multiple_of(b * (D // 2), D // 2), D // 2)
@@ -243,15 +269,33 @@
             def _():
                 stages[order](k - 2 * (k // (NB + 2)))
 
-    def accumulate(par, idx, first, value):
-        old = pacc[par, idx]
-        if first is not None:
-            old = jnp.where(first, 0.0, old)
-        pacc[par, idx] = old + value
+    def b_unit(lhs0, lhs1, tb, par, pb, first, u, values):
+        half_units = UNITS // 2
+        m, kq = u // half_units, u % half_units
+        rows = slice(m * (D // 2), (m + 1) * (D // 2))
+        lo = kq * KU
+        out_values = []
+        for idx, lhs in ((0, lhs0), (1, lhs1)):
+            value = values[idx] if kq else None
+            term = dot(lhs[tb * (T2 // T1) + lo // T1, rows, lo % T1:lo % T1 + KU], uu[2 * idx + pb][lo:lo + KU, :])
+            value = term if value is None else value + term
+            if kq == half_units - 1:
+                old = pacc[par, idx, rows, :]
+                if first is not None:
+                    old = jnp.where(first, 0.0, old)
+                pacc[par, idx, rows, :] = old + value
+            out_values.append(value)
+        return out_values
+
+    def b_some(lhs0, lhs1, tb, par, pb, first, rc, chunks, values):
+        for u in range(rc * UNITS // chunks, (rc + 1) * UNITS // chunks):
+            values = b_unit(lhs0, lhs1, tb, par, pb, first, u, values)
+        return values
 
     def b_part(lhs0, lhs1, tb, par, pb, first):
-        accumulate(par, 0, first, dot(lhs0[tb], uu[pb][...]))
-        accumulate(par, 1, first, dot(lhs1[tb], uu[2 + pb][...]))
+        values = None
+        for u in range(UNITS):
+            values = b_unit(lhs0, lhs1, tb, par, pb, first, u, values)
 
     def da3_store(f, par):
         return pltpu.make_async_copy(
@@ -265,15 +309,16 @@
         tb = lax.rem(before, N2)
         pp = lax.rem(before // N2 + 1, 2)
         w3j = w3[:, col]
-        w4j = w4[col, :]
-        for rc in range(T2 // RC):
-            rows = pl.ds(pl.multiple_of(t * T2 + rc * RC, RC), RC)
+        w4j = w4t[:, col]
+        values = None
+        for rc in range(T2 // RC2):
+            rows = pl.ds(pl.multiple_of(t * T2 + rc * RC2, RC2), RC2)
             a = dot(hn[rows, :], w3j).astype(bf16).astype(f32)
-            d = dot_nt(gn[rows, :], w4j)
+            d = dot(gn[rows, :], w4j)
             h, g = gelu_and_grad(a)
-            uu[par][rc * RC:(rc + 1) * RC, :] = h.astype(bf16)
-            uu[2 + par][rc * RC:(rc + 1) * RC, :] = (d * g).astype(bf16)
-        b_part(gt, ht, tb, pp, 1 - par, None if par == 0 else tb == 0)
+            uu[par][rc * RC2:(rc + 1) * RC2, :] = h.astype(bf16)
+            uu[2 + par][rc * RC2:(rc + 1) * RC2, :] = (d * g).astype(bf16)
+            values = b_some(gt, ht, tb, pp, 1 - par, None if par == 0 else tb == 0, rc, T2 // RC2, values)
 
     def l2_pair(k, carry):
         for par in (0, 1):
@@ -307,6 +352,10 @@
 
     da3_start(0, 0)
     da3_start(1, 1)
+    for cc in range(NB):
+        cols = slice(cc * FB, (cc + 1) * FB)
+        w4[cols, :] = w3[:, cols].T
+        w4t[:, cols] = w2[cols, :].T
 
     def dh2_pair(k, carry):
         comm(NB * N2 + k)
@@ -315,16 +364,17 @@
             for cc in range(NB):
                 da3_load(i, par, cc).wait()
             x_copy(i).wait()
-            rows = pl.ds(pl.multiple_of(i * T1, T1), T1)
-            lanes = pl.ds(pl.multiple_of(lax.rem(i, 4) * T1, T1), T1)
-            res = None
-            for cc in range(NB):
-                term = dot_nt(vv[2 * par + cc // 4, (cc % 4) * T1:(cc % 4 + 1) * T1, :], w3[:, cc * FB:(cc + 1) * FB])
-                res = term if res is None else res + term
-            dh2 = (res + gn[rows, :].astype(f32)).astype(bf16)
-            hn[rows, :] = dh2
-            ht[i // 4, :, lanes] = dh2.T
-            gt[i // 4, :, lanes] = xs[lax.rem(i, 4)].T
+            for m in (0, 1):
+                rows = pl.ds(pl.multiple_of(i * T1 + m * RH, RH), RH)
+                total = None
+                for cc in range(NB):
+                    lo = (cc % 4) * T1 + m * RH
+                    term = dot(vv[2 * par + cc // 4, lo:lo + RH, :], w4[cc * FB:(cc + 1) * FB, :])
+                    total = term if total is None else total + term
+                dh2 = (total + gn[rows, :].astype(f32)).astype(bf16)
+                hn[rows, :] = dh2
+                ht[i, :, m * RH:(m + 1) * RH] = dh2.T
+            gt[i] = xs[lax.rem(i, 4)].T
 
             @pl.when(i + 2 < N1)
             def _():
@@ -351,15 +401,16 @@
         tb = lax.rem(before, N2)
         pp = lax.rem(before // N2 + 1, 2)
         slot = lax.rem(f, 4)
-        w2j = w2[col, :]
-        for rc in range(T2 // RC):
-            rows = pl.ds(pl.multiple_of(t * T2 + rc * RC, RC), RC)
-            a = vv[slot, rc * RC:(rc + 1) * RC, :].astype(f32)
-            d = dot_nt(hn[rows, :], w2j)
+        w2j = w4t[:, col]
+        values = None
+        for rc in range(T2 // RC1):
+            rows = pl.ds(pl.multiple_of(t * T2 + rc * RC1, RC1), RC1)
+            a = vv[slot, rc * RC1:(rc + 1) * RC1, :].astype(f32)
+            d = dot(hn[rows, :], w2j)
             h, g = gelu_and_grad(a)
-            uu[par][rc * RC:(rc + 1) * RC, :] = h.astype(bf16)
-            uu[2 + par][rc * RC:(rc + 1) * RC, :] = (d * g).astype(bf16)
-        b_part(ht, gt, tb, pp, 1 - par, None if par == 0 else tb == 0)
+            uu[par][rc * RC1:(rc + 1) * RC1, :] = h.astype(bf16)
+            uu[2 + par][rc * RC1:(rc + 1) * RC1, :] = (d * g).astype(bf16)
+            values = b_some(ht, gt, tb, pp, 1 - par, None if par == 0 else tb == 0, rc, T2 // RC1, values)
 
     def l1_pair(k, carry):
         for par in (0, 1):
@@ -385,18 +436,35 @@
     lax.fori_loop(0, LAST_TRIP - base - NB * N2, tail, 0)
 
 
-def finish_kernel(piece, o1, o2, o3, o4):
-    p = pl.program_id(0)
-
-    @pl.when(p < NB)
-    def _():
-        o3[...] = piece[0, 1]
-        o4[...] = piece[0, 0].T
-
-    @pl.when(p >= NB)
-    def _():
-        o1[...] = piece[0, 1]
-        o2[...] = piece[0, 0].T
+def finish_kernel(sums, o1, o2, o3, o4, buf, flip, in_sem, wide_sem, tall_sem):
+    def load(p):
+        return pltpu.make_async_copy(sums.at[p], buf.at[p], in_sem.at[p])
+
+    def store_wide(o, j, p):
+        return pltpu.make_async_copy(
+            buf.at[p, 1], o.at[:, pl.ds(pl.multiple_of(j * FB, FB), FB)], wide_sem.at[p])
+
+    def store_tall(o, j, p):
+        return pltpu.make_async_copy(
+            flip.at[p], o.at[pl.ds(pl.multiple_of(j * FB, FB), FB), :], tall_sem.at[p])
+
+    for p in range(2 * NB):
+        load(p).start()
+    for base, wide, tall in ((0, o3, o4), (NB, o1, o2)):
+        def step(j, carry):
+            p = base + j
+            load(p).wait()
+            store_wide(wide, j, p).start()
+            flip[p] = buf[p, 0].T
+            store_tall(tall, j, p).start()
+            return carry
+        lax.fori_loop(0, NB, step, 0)
+    for base, wide, tall in ((0, o3, o4), (NB, o1, o2)):
+        def drain(j, carry):
+            store_wide(wide, j, base + j).wait()
+            store_tall(tall, j, base + j).wait()
+            return carry
+        lax.fori_loop(0, NB, drain, 0)
 
 
 def device_step(x_loc, g_loc, w_one, w_two, w_three, w_four):
@@ -413,13 +481,14 @@
         out_specs=(any_spec,) * 3,
         scratch_shapes=[
             pltpu.VMEM((N, D), bf16),
-            pltpu.VMEM((N2, D, T2), bf16),
+            pltpu.VMEM((N1, D, T1), bf16),
             pltpu.VMEM((N, D), bf16),
-            pltpu.VMEM((N2, D, T2), bf16),
+            pltpu.VMEM((N1, D, T1), bf16),
             pltpu.VMEM((D, F), bf16),
             pltpu.VMEM((F, D), bf16),
             pltpu.VMEM((D, F), bf16),
             pltpu.VMEM((F, D), bf16),
+            pltpu.VMEM((D, F), bf16),
             pltpu.VMEM((T2, FB), bf16),
             pltpu.VMEM((T2, FB), bf16),
             pltpu.VMEM((T2, FB), bf16),
@@ -449,15 +518,17 @@
     return pl.pallas_call(
         finish_kernel,
         name="finish",
-        grid=(2 * NB,),
         out_shape=(wide, tall, wide, tall),
-        in_specs=[pl.BlockSpec((1, 2, D, FB), lambda p: (p, 0, 0, 0))],
-        out_specs=(
-            pl.BlockSpec((D, FB), lambda p: (0, jnp.maximum(p - NB, 0))),
-            pl.BlockSpec((FB, D), lambda p: (jnp.maximum(p - NB, 0), 0)),
-            pl.BlockSpec((D, FB), lambda p: (0, jnp.minimum(p, NB - 1))),
-            pl.BlockSpec((FB, D), lambda p: (jnp.minimum(p, NB - 1), 0)),
-        ),
+        in_specs=[any_spec],
+        out_specs=(any_spec,) * 4,
+        scratch_shapes=[
+            pltpu.VMEM((2 * NB, 2, D, FB), f32),
+            pltpu.VMEM((2 * NB, FB, D), f32),
+            pltpu.SemaphoreType.DMA((2 * NB,)),
+            pltpu.SemaphoreType.DMA((2 * NB,)),
+            pltpu.SemaphoreType.DMA((2 * NB,)),
+        ],
+        compiler_params=pltpu.CompilerParams(vmem_limit_bytes=40 << 20),
     )(sums)
 
 

time: 319 us -> 276 us (0.87)
  Pallas kernels: 318 us -> 275 us
    pallas_call x1, Pallas kernels: 300 us -> 263 us  [device_step(): pl.pallas_call(kernel, name='grads', out_shape=(jax.ShapeDtypeStruct((2 *...]
    pallas_call x1, Pallas kernels: 18.3 us -> 12.1 us  [device_step(): pl.pallas_call(finish_kernel, name='finish', out_shape=(wide, tall, wide,...]
where the time goes in v3:
time: 276 us
  Pallas kernels  275 us (100%)
    pallas_call x1, Pallas kernels, device_step(): pl.pallas_call(kernel, name='grads', out_shape=(jax.ShapeDtypeStruct((2 *...  263 us
    pallas_call x1, Pallas kernels, device_step(): pl.pallas_call(finish_kernel, name='finish', out_shape=(wide, tall, wide,...  12.1 us

profile of v3, /device:TPU:0, one launch (start us, length us, event | category | flops | bytes accessed | tf_op | source)
XLA Modules:
  0.0 275.6 jit_solution(394151110957902852)
XLA Ops:
  0.6 262.6 %grads.1 = (f32[16,2,512,256]{3,2,1,0:T(8,128)}, bf16[8,8192,256]{2,1,0:T(8,128)(2,1)}, bf16[8,8192,256]{2,1,0:T(8,128)(2,1)}) custom-call(bf16[8192,512]{1,0:T(8,128)(2,1)} %x_hbm.1, bf16[8192,512]{1,0:T(8,128)(2,1)} %g_hbm.1, bf16[512,2048]{1,0:T(8,128)(2,1)} %w1_hbm.1, bf16[2048,512]{1,0:T(8,128)(2,1)} %w2_hbm.1, bf16[512,2048]{1,0:T(8,128)(2,1)} %w3_hbm.1, ...), custom_call_target="tpu_custom_call" | custom-call | flops 171798691840 | bytes 209715200 | tf_op jit(solution)/shard_map/grads/pallas_call | solution.py:472
  263.2 12.1 %finish.1 = (f32[512,2048]{1,0:T(8,128)}, f32[2048,512]{1,0:T(8,128)}, f32[512,2048]{1,0:T(8,128)}, f32[2048,512]{1,0:T(8,128)}) custom-call(f32[16,2,512,256]{3,2,1,0:T(8,128)} %get-tuple-element.5.sums), custom_call_target="tpu_custom_call" | custom-call | tf_op jit(solution)/shard_map/finish/pallas_call | solution.py:518
